TPU v7x, 512 devices: a 4x2x32 block of a 4x8x32 slice. The times are simulated.
512 devices in a mesh: groups: 2 (over y), seq: 32 (over z), sample: 4 (over x), vocab: 2 (over core).
Axes of the slice: x: 4, y: 2, z: 32, core: 2. Of those that a mesh axis runs over, the one named last changes fastest.
The devices are a block of a 4x8x32 slice.
Arguments:
- queries: bfloat16 [16, 2048, 1792], P(('groups', 'sample'), 'seq', 'vocab'), parts along dimension 0, may hold values from -130 to 130
- key_states: bfloat16 [16, 2048, 256], P(('groups', 'sample'), 'seq', 'vocab'), parts along dimension 0, may hold values from -8 to 8
- value_states: bfloat16 [16, 2048, 256], P(('groups', 'sample'), 'seq', 'vocab'), parts along dimension 0, may hold values from -6 to 6
- residual: bfloat16 [16, 2048, 1792], P(('groups', 'sample'), 'seq'), parts along dimension 0, may hold values from -3 to 3
- out_weight: bfloat16 [1792, 1792], P('vocab'), may hold values from -0.5 to 0.5
- norm_gain: float32 [1792], replicated, may hold values from 0.5 to 1.5
- vocab_head: bfloat16 [81920, 1792], P(('seq', 'sample', 'vocab')), may hold values from -21 to 21
- targets: int32 [16, 2048], P(('groups', 'sample')), parts along dimension 0, may hold values from 0 to 81919
- scored_slots: int32 [16, 512], P(('groups', 'sample')), parts along dimension 0, may hold values from -1 to 2047, as said below
- lengths: int32 [16], P(('groups', 'sample')), parts along dimension 0, may hold values from 512 to 2048
- rewards: int32 [16], P(('groups', 'sample')), parts along dimension 0, may hold values from 0 to 4
Outputs:
- token_logprobs: float32 [16, 512], P(('groups', 'sample'), 'seq'), parts along dimension 0
- seq_scores: float32 [16], P(('groups', 'sample')), parts along dimension 0
- advantages: float32 [16], P(('groups', 'sample')), parts along dimension 0
- objective: float32 [2], P('groups'), parts along dimension 0
There are 2 independent parts, one for each index of `groups`. A program takes and returns all parts, laid end to end along the dimension named above; an argument that names none is the same for every part. Nothing has to cross between parts.
Inputs may be any that keep to these rules, and one draw needn't show every extreme that they name: `scored_slots`: slots b * 16 to (b + 1) * 16 - 1 of a completion hold distinct positions of b * 64 to (b + 1) * 64 - 1 in rising order, followed by -1 in unused slots; every completion fills all 16 slots of some block; positions not listed are not scored. Positions from lengths[i] on are padding.
All inputs are finite; a program needn't handle non-finite values.
Results may differ from a plain program's by a relative error of at most 0.0085.
Values may be sent and summed in bfloat16 or wider, within the bound.
A program may use at most 64 MiB of HBM per device.

v0:
```python
import jax
import jax.numpy as jnp
from jax import lax
from jax.sharding import PartitionSpec as P

HD = 128
K = 8
floor_value = -1e30


def side_by_side(arrays, axis, dim, along):
    both = jnp.concatenate(arrays, axis=along)
    whole, at, gathered = (lax.all_gather(both, axis, axis=dim, tiled=True), 0, [])
    for a in arrays:
        gathered.append(lax.slice_in_dim(whole, at, at + a.shape[along], axis=along))
        at += a.shape[along]
    return tuple(gathered)


def sent_to_all(value, axis):
    copies = jnp.broadcast_to(value, (lax.axis_size(axis), *value.shape))
    return lax.all_to_all(copies, axis, split_axis=0, concat_axis=0, tiled=True)


def taken_together(value, axis):
    return sent_to_all(value, axis).astype(jnp.float32).sum(axis=0)


def all_in_one(value, axis):
    leaves = jax.tree.leaves(value)
    turns = sorted(range(len(leaves)), key=lambda k: -leaves[k].size)
    width = (1, *leaves[turns[0]].shape)[-1]
    lines = [
        jnp.pad(leaves[k].reshape(-1), (0, -leaves[k].size % width)).reshape(-1, width)
        for k in turns
    ]
    both, at, found = (lax.all_gather(jnp.concatenate(lines), axis), 0, {})
    for k, line in zip(turns, lines):
        slab = both[:, at : at + len(line)].reshape(len(both), -1)
        found[k] = slab[:, : leaves[k].size].reshape(-1, *leaves[k].shape)
        at += len(line)
    numbers = iter(range(len(leaves)))
    return jax.tree.map(lambda _: found[next(numbers)], value)


def joined(value, axis, combine):
    everything = all_in_one(value, axis)
    initial = jax.tree.map(lambda part: part[0], everything)

    def turn(k, so_far):
        return combine(so_far, jax.tree.map(lambda part: part[k], everything))

    return lax.fori_loop(1, lax.axis_size(axis), turn, initial)


def rms_scale(hidden, norm_gain):
    power = jnp.mean(hidden * hidden, axis=-1, keepdims=True)
    return (hidden * lax.rsqrt(power + 1e-06) * norm_gain).astype(jnp.bfloat16)


def merge_stats(left, right):
    top_score = jnp.maximum(left[0], right[0])
    weight_sum = left[1] * jnp.exp(left[0] - top_score) + right[1] * jnp.exp(right[0] - top_score)
    return (top_score, weight_sum, left[2] + right[2])


def shards(
    queries,
    key_states,
    value_states,
    residual,
    out_weight,
    norm_gain,
    vocab_head,
    targets,
    scored_slots,
    lengths,
    rewards,
):
    sample_count, block_len, query_width = queries.shape
    kv_heads = key_states.shape[2] // HD
    group_size = query_width // HD // kv_heads
    model_width = out_weight.shape[1]
    full_len = targets.shape[1]
    slot_total = scored_slots.shape[1]
    slot_cap = slot_total // lax.axis_size("seq")
    first_pos = lax.axis_index("seq") * block_len
    query_pos = first_pos + jnp.arange(block_len, dtype=jnp.int32)
    query_view = queries.reshape(sample_count, block_len, kv_heads, group_size, HD)
    stat_shape = (sample_count, block_len, kv_heads, group_size)
    pieces = side_by_side((key_states, value_states), "seq", 1, 0)
    top_score = jnp.full(stat_shape, floor_value, jnp.float32)
    piece_len = pieces[0].shape[1]
    key_view = pieces[0].reshape(sample_count, piece_len, kv_heads, HD)
    value_view = pieces[1].reshape(sample_count, piece_len, kv_heads, HD)
    scores = jnp.einsum(
        "srkgd,snkd->srkgn", query_view, key_view, preferred_element_type=jnp.float32
    ) * HD ** (-0.5)
    key_pos = jnp.arange(piece_len, dtype=jnp.int32)
    allowed = (key_pos[None, :] <= query_pos[:, None])[None, :, None, None, :]
    masked = jnp.where(allowed, scores, floor_value)
    new_top = jnp.maximum(top_score, jnp.max(masked, axis=-1))
    weights = jnp.where(allowed, jnp.exp(masked - new_top[..., None]), 0.0)
    weight_sum = jnp.sum(weights, axis=-1)
    update = jnp.einsum(
        "srkgn,snkd->srkgd",
        weights.astype(jnp.bfloat16),
        value_view,
        preferred_element_type=jnp.float32,
    )
    weighted = update
    new_top, weight_sum, weighted = (new_top, weight_sum, weighted)
    safe_sum = jnp.where(weight_sum > 0, weight_sum, 1.0)
    attended = (
        (weighted / safe_sum[..., None])
        .reshape(sample_count, block_len, query_width)
        .astype(jnp.bfloat16)
    )
    own_slots = lax.dynamic_slice_in_dim(
        scored_slots, lax.axis_index("seq") * slot_cap, slot_cap, 1
    )
    local_pos = jnp.clip(own_slots - first_pos, 0, block_len - 1)
    picked_attended = jnp.take_along_axis(attended, local_pos[:, :, None], axis=1)
    picked_resid = jnp.take_along_axis(residual, local_pos[:, :, None], axis=1)
    partial_value = jnp.einsum(
        "scq,qd->scd", picked_attended, out_weight, preferred_element_type=jnp.float32
    )
    head_rows = lax.all_gather(vocab_head, "sample", axis=0, tiled=True)
    shard_rows = vocab_head.shape[0]
    row_index = jnp.arange(head_rows.shape[0], dtype=jnp.int32)
    owner = (
        lax.axis_index("seq") * lax.axis_size("sample") + row_index // shard_rows
    ) * lax.axis_size("vocab") + lax.axis_index("vocab")
    vocab_ids = owner * shard_rows + row_index % shard_rows
    summed = taken_together(partial_value.astype(jnp.bfloat16), "vocab").astype(jnp.float32)
    normed = rms_scale(picked_resid.astype(jnp.float32) + summed, norm_gain)
    pieces = lax.all_gather(normed, "seq", axis=1, tiled=True)
    piece_len = pieces.shape[1]
    flat = pieces.reshape(sample_count * piece_len, model_width)
    logits = lax.dot_general(
        flat, head_rows, (((1,), (1,)), ((), ())), preferred_element_type=jnp.float32
    )
    logits = logits.reshape(sample_count, piece_len, head_rows.shape[0])
    top_local = jnp.max(logits, axis=-1)
    sum_local = jnp.sum(jnp.exp(logits - top_local[..., None]), axis=-1)
    slot_piece = jnp.maximum(scored_slots, 0)
    wanted = jnp.take_along_axis(targets, slot_piece, axis=1)
    picked = jnp.sum(jnp.where(vocab_ids[None, None, :] == wanted[..., None], logits, 0.0), axis=-1)
    top_local, sum_local, pick_local = (top_local, sum_local, picked)
    top_all, sum_all, pick_all = joined(
        (top_local, sum_local, pick_local), ("seq", "vocab"), merge_stats
    )
    logprob = pick_all - (top_all + jnp.log(sum_all))
    scored = (scored_slots >= 0) & (scored_slots < lengths[:, None])
    token_all = jnp.where(scored, logprob, 0.0)
    own_scores = jnp.sum(token_all, axis=-1) / full_len
    own_tokens = lax.dynamic_slice_in_dim(token_all, lax.axis_index("seq") * slot_cap, slot_cap, 1)
    own_reward = rewards.astype(jnp.float32)
    reward_all, score_all = (
        lax.all_gather(own_reward, "sample", axis=0, tiled=True),
        lax.all_gather(own_scores, "sample", axis=0, tiled=True),
    )
    reward_sum = jnp.sum(reward_all)
    own_advantage = own_reward - (reward_sum - own_reward) / (K - 1)
    every_advantage = reward_all - (reward_sum - reward_all) / (K - 1)
    objective = -(jnp.sum(every_advantage * score_all) / K).reshape(1)
    return (own_tokens, own_scores, own_advantage, objective)


def solution(mesh):
    in_specs = (
        P(("groups", "sample"), "seq", "vocab"),
        P(("groups", "sample"), "seq", "vocab"),
        P(("groups", "sample"), "seq", "vocab"),
        P(("groups", "sample"), "seq", None),
        P("vocab", None),
        P(),
        P(("seq", "sample", "vocab"), None),
        P(("groups", "sample"), None),
        P(("groups", "sample"), None),
        P(("groups", "sample")),
        P(("groups", "sample")),
    )
    out_specs = (
        P(("groups", "sample"), "seq"),
        P(("groups", "sample")),
        P(("groups", "sample")),
        P("groups"),
    )
    return jax.shard_map(shards, mesh=mesh, in_specs=in_specs, out_specs=out_specs, check_vma=False)
```

profile of v0, /device:TPU:40, one launch (start us, length us, event | category | flops | bytes accessed | tf_op | source)
XLA Modules:
  0.0 512.0 jit_solution(15304321632450815917)
XLA Ops:
  7.3 1.5 pad_maximum_fusion
  8.9 0.7 all-gather.10.cloned.1.call-update
  9.8 0.8 compare_and_fusion
  10.6 2.6 gather_fusion
  13.4 157.4 %all-gather.6.cloned.1.call-done = bf16[4,2048,128]{2,1,0:T(8,128)(2,1)} async-done(((bf16[4,64,128]{2,1,0:T(8,128)(2,1)}), bf16[4,2048,128]{2,1,0:T(8,128)(2,1)}) %all-gather.6.cloned.1.call-update) | async-done | bytes 2097168 | tf_op jit(solution)/shard_map/all_gather | solution.py:13
  170.8 2.7 fusion.2
  173.5 2.2 fusion.3
  175.7 1.6 fusion.26
  177.3 0.9 copy.21
  178.2 1.2 convert_element_type.31
  179.4 0.8 gather_fusion.1
  180.9 3.9 all_to_all.5
  185.1 0.8 multiply_convert_fusion
  186.0 9.1 %gather_fusion.2 = s32[1024]{0:T(1024)S(1)} fusion(s32[2,2048]{1,0:T(2,128)S(1)} %copy-done.1, s32[1024]{0:T(1024)S(1)} %bitcast.125), kind=kCustom, calls=%fused_computation.2 | custom fusion | bytes 16384 | tf_op jit(solution)/shard_map/jit(take_along_axis)/gather | solution.py:147
  195.1 1.3 dynamic-slice
  197.2 34.9 %all-gather.10.cloned.1.call-done = bf16[1280,1792]{1,0:T(8,128)(2,1)} async-done(((bf16[320,1792]{1,0:T(8,128)(2,1)}), bf16[1280,1792]{1,0:T(8,128)(2,1)}) %all-gather.10.cloned.1.call-update) | async-done | bytes 4587536 | tf_op jit(solution)/shard_map/all_gather | solution.py:128
  232.1 142.7 %all-gather.8.cloned.1.call-done = bf16[2,512,1792]{2,1,0:T(8,128)(2,1)} async-done(((bf16[2,16,1792]{2,1,0:T(8,128)(2,1)}), bf16[2,512,1792]{2,1,0:T(8,128)(2,1)}) %all-gather.8.cloned.1.call-update) | async-done | bytes 3670032 | tf_op jit(solution)/shard_map/all_gather | solution.py:137
  374.7 8.5 %fusion.54 = (f32[2,512]{1,0:T(2,128)S(1)}, f32[2,512,1280]{2,1,0:T(8,128)S(1)}) fusion(bf16[2,512,1792]{2,1,0:T(8,128)(2,1)} %all-gather.8.cloned.1.call-done, bf16[1280,1792]{1,0:T(8,128)(2,1)} %all-gather.10.cloned.1.call-done), kind=kOutput, calls=%fused_computation.86 | convolution fusion | flops 4698930176 | bytes 13504512 | tf_op jit(solution)/shard_map/dot_general | solution.py:140
  383.2 1.5 exponential_reduce_fusion
  384.8 57.0 %all-gather.1 = f32[64,6,512]{2,1,0:T(8,128)S(1)} all-gather(f32[1,6,512]{2,1,0:T(8,128)S(1)} %maximum_bitcast_fusion), channel_id=2, replica_groups=mesh['groups'=2,'seq'=32,'sample'=4,'vocab'=2] {'seq','vocab'}, dimensions={0}, use_global_device_ids=true | all-gather | bytes 798720 | tf_op jit(solution)/shard_map/all_gather | solution.py:37
  441.7 1.1 fusion.53
  442.8 46.1 %while.19 = (s32[]{:T(128)}, f32[2,512]{1,0:T(2,128)S(1)}, f32[2,512]{1,0:T(2,128)S(1)}, f32[2,512]{1,0:T(2,128)S(1)}, f32[64,2,512]{2,1,0:T(2,128)}, /*index=5*...) while((s32[]{:T(128)}, f32[2,512]{1,0:T(2,128)S(1)}, ...), condition=%wide.region_8.9_spmd, body=%wide.region_7.8_spmd.sunk | while | flops 7173 | bytes 37011 | solution.py:53
  443.5 0.7 fusion.58
  444.2 0.7 fusion.58
  445.0 0.7 fusion.58
  446.4 0.7 fusion.58
  447.9 0.7 fusion.58
  448.6 0.7 fusion.58
  449.4 0.7 fusion.58
  452.3 0.7 fusion.58
  453.0 0.7 fusion.58
  453.7 0.7 fusion.58
  454.5 0.7 fusion.58
  455.2 0.8 fusion.58
  456.0 0.7 fusion.58
  456.7 0.7 fusion.58
  457.5 0.7 fusion.58
  458.2 0.7 fusion.58
  459.0 0.7 fusion.58
  459.7 0.7 fusion.58
  461.2 0.7 fusion.58
  461.9 0.7 fusion.58
  463.4 0.7 fusion.58
  466.3 0.7 fusion.58
  467.7 0.7 fusion.58
  468.4 0.7 fusion.58
  469.9 0.7 fusion.58
  471.4 0.7 fusion.58
  472.1 0.7 fusion.58
  473.5 0.7 fusion.58
  474.3 0.7 fusion.58
  475.7 0.7 fusion.58
  476.5 0.7 fusion.58
  477.2 0.7 fusion.58
  478.7 0.7 fusion.58
  479.4 0.7 fusion.58
  481.7 0.7 fusion.58
  483.1 0.7 fusion.58
  483.8 0.7 fusion.58
  487.5 0.7 fusion.58
  488.2 0.7 fusion.58
  489.7 10.3 %all-reduce.2 = (f32[8]{0:T(128)S(1)}, f32[8]{0:T(128)S(1)}) all-reduce(f32[8]{0:T(128)S(1)} %convert_dynamic-update-slice_fusion, f32[8]{0:T(128)S(1)} %get-tuple-element.205), channel_id=1, replica_groups=mesh['groups'=2,'seq'=32,'sample'=4,'vocab'=2] {'sample'}, use_global_device_ids=true, to_apply=%add | all-reduce | flops 16 | bytes 128
  500.6 1.2 multiply_subtract_fusion
  501.8 1.2 multiply_reduce_fusion.1
  (70 shorter events, 20.6 us)
Async XLA Ops:
  7.2 173.1 %copy-start = (bf16[896,1792]{1,0:T(8,128)(2,1)S(1)}, bf16[896,1792]{1,0:T(8,128)(2,1)}, u32[]{:S(2)}) copy-start(bf16[896,1792]{1,0:T(8,128)(2,1)} %param.17) | copy-start | bytes 9633796
  7.2 163.6 %all-gather.6.cloned.1.call-start = ((), (), s32[]{:S(2)}) async-start(), calls=%async_computation.1 | async-start | bytes 2162688 | tf_op jit(solution)/shard_map/all_gather | solution.py:13
  8.9 223.2 %all-gather.10.cloned.1.call-start = ((), (), s32[]{:S(2)}) async-start(), calls=%async_computation.3 | async-start | bytes 5734400 | tf_op jit(solution)/shard_map/all_gather | solution.py:128
  9.7 365.0 %all-gather.8.cloned.1.call-start = ((), (), s32[]{:S(2)}) async-start(), calls=%async_computation.2 | async-start | bytes 3784704 | tf_op jit(solution)/shard_map/all_gather | solution.py:137
  173.5 2.3 copy-start.3
  177.3 7.8 %copy-start.5 = (f32[1792]{0:T(1024)S(1)}, f32[1792]{0:T(1024)}, u32[]{:S(2)}) copy-start(f32[1792]{0:T(1024)} %param.18) | copy-start | bytes 21508
  177.3 8.6 %copy-start.4 = (s32[2,512]{1,0:T(2,128)S(1)}, s32[2,512]{1,0:T(2,128)}, u32[]{:S(2)}) copy-start(s32[2,512]{1,0:T(2,128)} %param.21) | copy-start | bytes 12292
  177.3 8.6 %copy-start.1 = (s32[2,2048]{1,0:T(2,128)S(1)}, s32[2,2048]{1,0:T(2,128)}, u32[]{:S(2)}) copy-start(s32[2,2048]{1,0:T(2,128)} %param.20) | copy-start | bytes 49156
  180.3 4.6 copy-start.2
  180.3 16.8 %copy-start.7 = (s32[2]{0:T(128)S(1)}, s32[2]{0:T(128)}, u32[]{:S(2)}) copy-start(s32[2]{0:T(128)} %param.23) | copy-start | bytes 28
  383.2 105.7 %copy-start.6 = (s32[2]{0:T(128)S(1)}, s32[2]{0:T(128)}, u32[]{:S(2)}) copy-start(s32[2]{0:T(128)} %param.22) | copy-start | bytes 28
Sparse Core Ops, SparseCore 0:
  10.1 160.6 all-gather.5
  172.9 59.0 all-gather.9
  234.2 140.4 all-gather.7
where the time goes:
time: 517 us; the launch traced here: 512 us
  waiting for transfers between devices  336 us (65%)
  blocking collectives  71.2 us (14%)
  other arithmetic  56.3 us (11%)
  local copies, waits for them, and re-layouts  17.8 us (3%)
  between operations  16.5 us (3%)
  matrix products  13.3 us (3%)
    all_gather x1, waiting for transfers between devices, side_by_side(): lax.all_gather(both, axis, axis=dim, tiled=True)  157 us
    all_gather x1, waiting for transfers between devices, shards(): pieces = lax.all_gather(normed, 'seq', axis=1, tiled=True)  143 us
    all_gather x1, blocking collectives, all_in_one(): both, at, found = (lax.all_gather(jnp.concatenate(lines), axis), 0, {})  57 us
    add x63, other arithmetic, merge_stats(): left[1] * jnp.exp(left[0] - top_score)  45.2 us
    all_gather x1, waiting for transfers between devices, shards(): head_rows = lax.all_gather(vocab_head, 'sample', axis=0, tiled=True)  34.9 us
  transfers between devices with their start and end apart: 3, of which 3 were waited for; matrix products, arithmetic and copies ran while one was open for 5% of the time, Pallas kernels for 0%

commit v1 on v0

--- a/solution.py
+++ b/solution.py
@@ -125,7 +125,19 @@
     partial_value = jnp.einsum(
         "scq,qd->scd", picked_attended, out_weight, preferred_element_type=jnp.float32
     )
-    head_rows = lax.all_gather(vocab_head, "sample", axis=0, tiled=True)
+    arr_out = lax.psum(1, "sample")
+    wide_out = lax.axis_index("sample")
+    carry_in, x_new, reached = (arr_out, wide_out, vocab_head.shape[0])
+    head_rows = jnp.zeros(
+        (*vocab_head.shape[:0], carry_in * reached, *vocab_head.shape[0 + 1 :]), vocab_head.dtype
+    )
+    upper = vocab_head
+    buffer = [(j, (j + 1) % carry_in) for j in range(carry_in)]
+    for s in range(carry_in):
+        before = (x_new - s) % carry_in
+        head_rows = lax.dynamic_update_slice_in_dim(head_rows, upper, before * reached, axis=0)
+        if s < carry_in - 1:
+            upper = lax.ppermute(upper, axis_name="sample", perm=buffer)
     shard_rows = vocab_head.shape[0]
     row_index = jnp.arange(head_rows.shape[0], dtype=jnp.int32)
     owner = (

time: 517 us -> 460 us (0.89)
  waiting for transfers between devices: 336 us -> 260 us
  local copies, waits for them, and re-layouts: 17.8 us -> 28.3 us
  starting transfers between devices: 0.19 us -> 8.1 us
    all_gather x1, waiting for transfers between devices: 143 us -> 39.3 us  [shards(): pieces = lax.all_gather(normed, 'seq', axis=1, tiled=True)]
    ppermute x0 -> x3, waiting for transfers between devices: none -> 62.2 us  [shards(): upper = lax.ppermute(upper, axis_name='sample', perm=buffer)]
    all_gather x1 -> x0, waiting for transfers between devices: 34.9 us -> none  [shards(): head_rows = lax.all_gather(vocab_head, 'sample', axis=0, tiled=True)]
    dynamic_update_slice x0 -> x4, local copies, waits for them, and re-layouts: none -> 8.15 us  [shards(): lax.dynamic_update_slice_in_dim(head_rows, upper, before * reached, axis=0)]
    ppermute x0 -> x3, starting transfers between devices: none -> 7.97 us  [shards(): upper = lax.ppermute(upper, axis_name='sample', perm=buffer)]
  transfers between devices with their start and end apart: 3 -> 5, of which waited for: 3 -> 5; matrix products, arithmetic and copies ran while one was open for 5% -> 5% of each run, Pallas kernels for 0% -> 0%
where the time goes in v1:
time: 460 us; the launch traced here: 455 us
  waiting for transfers between devices  260 us (57%)
  blocking collectives  70.9 us (15%)
  other arithmetic  56.5 us (12%)
  local copies, waits for them, and re-layouts  28.3 us (6%)
  between operations  16.9 us (4%)
  matrix products  13.3 us (3%)
  starting transfers between devices  8.1 us (2%)
    all_gather x1, waiting for transfers between devices, side_by_side(): lax.all_gather(both, axis, axis=dim, tiled=True)  158 us
    ppermute x3, waiting for transfers between devices, shards(): upper = lax.ppermute(upper, axis_name='sample', perm=buffer)  62.2 us
    all_gather x1, blocking collectives, all_in_one(): both, at, found = (lax.all_gather(jnp.concatenate(lines), axis), 0, {})  56.3 us
    add x63, other arithmetic, merge_stats(): left[1] * jnp.exp(left[0] - top_score)  45.2 us
    all_gather x1, waiting for transfers between devices, shards(): pieces = lax.all_gather(normed, 'seq', axis=1, tiled=True)  39.3 us
    unnamed x1, blocking collectives  10.6 us
  transfers between devices with their start and end apart: 5, of which 5 were waited for; matrix products, arithmetic and copies ran while one was open for 5% of the time, Pallas kernels for 0%

profile of v1, /device:TPU:40, one launch (start us, length us, event | category | flops | bytes accessed | tf_op | source)
XLA Modules:
  0.0 454.8 jit_solution(3630867505777340210)
XLA Ops:
  7.3 1.6 pad_maximum_fusion
  9.0 0.8 compare_and_fusion
  9.8 2.6 gather_fusion
  12.6 158.2 %all-gather.5.cloned.1.call-done = bf16[4,2048,128]{2,1,0:T(8,128)(2,1)} async-done(((bf16[4,64,128]{2,1,0:T(8,128)(2,1)}), bf16[4,2048,128]{2,1,0:T(8,128)(2,1)}) %all-gather.5.cloned.1.call-update) | async-done | bytes 2097168 | tf_op jit(solution)/shard_map/all_gather | solution.py:13
  170.8 2.6 fusion.2
  173.5 2.2 fusion.3
  175.7 1.6 fusion.26
  177.3 0.8 copy.21
  178.2 1.2 convert_element_type.31
  179.4 0.8 gather_fusion.1
  180.9 3.9 all_to_all.5
  185.0 0.8 multiply_convert_fusion
  185.9 3.7 collective-permute-start
  189.5 27.2 %collective-permute-done = bf16[320,1792]{1,0:T(8,128)(2,1)} collective-permute-done((bf16[320,1792]{1,0:T(8,128)(2,1)}, bf16[320,1792]{1,0:T(8,128)(2,1)}, u32[]{:S(2)}, u32[]{:S(2)}) %collective-permute-start) | collective-permute-done | bytes 1146912 | tf_op jit(solution)/shard_map/ppermute | solution.py:140
  216.7 2.4 collective-permute-start.1
  219.1 1.3 dynamic-slice
  221.0 25.6 %collective-permute-done.1 = bf16[320,1792]{1,0:T(8,128)(2,1)} collective-permute-done((bf16[320,1792]{1,0:T(8,128)(2,1)}, bf16[320,1792]{1,0:T(8,128)(2,1)}, u32[]{:S(2)}, u32[]{:S(2)}) %collective-permute-start.1) | collective-permute-done | bytes 1146912 | tf_op jit(solution)/shard_map/ppermute | solution.py:140
  246.6 1.9 collective-permute-start.2
  248.9 9.1 %gather_fusion.2 = s32[1024]{0:T(1024)S(1)} fusion(s32[2,2048]{1,0:T(2,128)S(1)} %copy-done.1, s32[1024]{0:T(1024)S(1)} %bitcast.125), kind=kCustom, calls=%fused_computation.2 | custom fusion | bytes 16384 | tf_op jit(solution)/shard_map/jit(take_along_axis)/gather | solution.py:159
  258.1 2.4 broadcast_in_dim.82
  260.5 1.1 constant_dynamic-update-slice_fusion.3
  261.6 2.4 constant_dynamic-update-slice_fusion.2
  263.9 2.3 constant_dynamic-update-slice_fusion.1
  266.3 9.5 %collective-permute-done.2 = bf16[320,1792]{1,0:T(8,128)(2,1)} collective-permute-done((bf16[320,1792]{1,0:T(8,128)(2,1)}, bf16[320,1792]{1,0:T(8,128)(2,1)}, u32[]{:S(2)}, u32[]{:S(2)}) %collective-permute-start.2) | collective-permute-done | bytes 1146912 | tf_op jit(solution)/shard_map/ppermute | solution.py:140
  275.7 2.4 constant_dynamic-update-slice_fusion
  278.1 39.3 %all-gather.7.cloned.1.call-done = bf16[2,512,1792]{2,1,0:T(8,128)(2,1)} async-done(((bf16[2,16,1792]{2,1,0:T(8,128)(2,1)}), bf16[2,512,1792]{2,1,0:T(8,128)(2,1)}) %all-gather.7.cloned.1.call-update) | async-done | bytes 3670032 | tf_op jit(solution)/shard_map/all_gather | solution.py:149
  317.4 8.5 %fusion.56 = (f32[2,512]{1,0:T(2,128)S(1)}, f32[2,512,1280]{2,1,0:T(8,128)S(1)}) fusion(bf16[2,512,1792]{2,1,0:T(8,128)(2,1)} %all-gather.7.cloned.1.call-done, bf16[1280,1792]{1,0:T(8,128)(2,1)} %constant_dynamic-update-slice_fusion), kind=kOutput, calls=%fused_computation.93 | convolution fusion | flops 4698930176 | bytes 13504512 | tf_op jit(solution)/shard_map/dot_general | solution.py:152
  325.9 1.5 exponential_reduce_fusion
  327.5 56.3 %all-gather.1 = f32[64,6,512]{2,1,0:T(8,128)S(1)} all-gather(f32[1,6,512]{2,1,0:T(8,128)S(1)} %maximum_bitcast_fusion), channel_id=2, replica_groups=mesh['groups'=2,'seq'=32,'sample'=4,'vocab'=2] {'seq','vocab'}, dimensions={0}, use_global_device_ids=true | all-gather | bytes 798720 | tf_op jit(solution)/shard_map/all_gather | solution.py:37
  383.8 1.1 fusion.55
  384.9 46.1 %while.19 = (s32[]{:T(128)}, f32[2,512]{1,0:T(2,128)S(1)}, f32[2,512]{1,0:T(2,128)S(1)}, f32[2,512]{1,0:T(2,128)S(1)}, f32[64,2,512]{2,1,0:T(2,128)}, /*index=5*...) while((s32[]{:T(128)}, f32[2,512]{1,0:T(2,128)S(1)}, ...), condition=%wide.region_8.9_spmd, body=%wide.region_7.8_spmd.sunk | while | flops 7173 | bytes 37011 | solution.py:53
  385.6 0.7 fusion.60
  386.3 0.7 fusion.60
  387.1 0.7 fusion.60
  388.5 0.7 fusion.60
  390.0 0.7 fusion.60
  390.7 0.7 fusion.60
  391.4 0.7 fusion.60
  395.1 0.7 fusion.60
  395.8 0.7 fusion.60
  396.6 0.7 fusion.60
  397.3 0.8 fusion.60
  398.8 0.7 fusion.60
  399.6 0.7 fusion.60
  400.3 0.7 fusion.60
  401.1 0.7 fusion.60
  401.8 0.7 fusion.60
  403.3 0.7 fusion.60
  405.5 0.7 fusion.60
  408.4 0.7 fusion.60
  409.8 0.7 fusion.60
  410.5 0.7 fusion.60
  413.5 0.7 fusion.60
  415.6 0.7 fusion.60
  416.4 0.7 fusion.60
  417.8 0.7 fusion.60
  419.3 0.7 fusion.60
  420.8 0.7 fusion.60
  421.5 0.7 fusion.60
  423.7 0.7 fusion.60
  429.6 0.7 fusion.60
  432.4 10.6 %all-reduce.2 = (f32[8]{0:T(128)S(1)}, f32[8]{0:T(128)S(1)}) all-reduce(f32[8]{0:T(128)S(1)} %convert_dynamic-update-slice_fusion, f32[8]{0:T(128)S(1)} %get-tuple-element.205), channel_id=1, replica_groups=mesh['groups'=2,'seq'=32,'sample'=4,'vocab'=2] {'sample'}, use_global_device_ids=true, to_apply=%add | all-reduce | flops 16 | bytes 128
  443.6 1.2 multiply_subtract_fusion
  444.8 1.3 multiply_reduce_fusion.1
  (80 shorter events, 27.1 us)
Async XLA Ops:
  7.2 173.1 %copy-start = (bf16[896,1792]{1,0:T(8,128)(2,1)S(1)}, bf16[896,1792]{1,0:T(8,128)(2,1)}, u32[]{:S(2)}) copy-start(bf16[896,1792]{1,0:T(8,128)(2,1)} %param.17) | copy-start | bytes 9633796
  7.2 163.6 %all-gather.5.cloned.1.call-start = ((), (), s32[]{:S(2)}) async-start(), calls=%async_computation.1 | async-start | bytes 2162688 | tf_op jit(solution)/shard_map/all_gather | solution.py:13
  8.9 308.6 %all-gather.7.cloned.1.call-start = ((), (), s32[]{:S(2)}) async-start(), calls=%async_computation.2 | async-start | bytes 3784704 | tf_op jit(solution)/shard_map/all_gather | solution.py:149
  173.5 2.3 copy-start.4
  177.3 7.7 %copy-start.6 = (f32[1792]{0:T(1024)S(1)}, f32[1792]{0:T(1024)}, u32[]{:S(2)}) copy-start(f32[1792]{0:T(1024)} %param.18) | copy-start | bytes 21508
  177.3 43.7 %copy-start.5 = (s32[2,512]{1,0:T(2,128)S(1)}, s32[2,512]{1,0:T(2,128)}, u32[]{:S(2)}) copy-start(s32[2,512]{1,0:T(2,128)} %param.21) | copy-start | bytes 12292
  177.3 71.3 %copy-start.8 = (s32[2]{0:T(128)S(1)}, s32[2]{0:T(128)}, u32[]{:S(2)}) copy-start(s32[2]{0:T(128)} %param.23) | copy-start | bytes 28
  177.3 71.6 %copy-start.1 = (s32[2,2048]{1,0:T(2,128)S(1)}, s32[2,2048]{1,0:T(2,128)}, u32[]{:S(2)}) copy-start(s32[2,2048]{1,0:T(2,128)} %param.20) | copy-start | bytes 49156
  180.2 4.6 %copy-start.3 = (bf16[32,1792]{1,0:T(8,128)(2,1)S(1)}, bf16[32,1792]{1,0:T(8,128)(2,1)}, u32[]{:S(2)}) copy-start(bf16[32,1792]{1,0:T(8,128)(2,1)} %gather_fusion) | copy-start | bytes 344068
  185.9 30.8 %collective-permute-start = (bf16[320,1792]{1,0:T(8,128)(2,1)}, bf16[320,1792]{1,0:T(8,128)(2,1)}, u32[]{:S(2)}, u32[]{:S(2)}) collective-permute-start(bf16[320,1792]{1,0:T(8,128)(2,1)} %param.19), channel_id=1, source_target_pairs={{0,2},{2,4},{4,6},{6,0},{1,3},{3,5},{5,7},{7,1},{8,10},{10,12},{12... | collective-permute-start | bytes 3440648 | tf_op jit(solution)/shard_map/ppermute | solution.py:140
  216.7 29.9 %collective-permute-start.1 = (bf16[320,1792]{1,0:T(8,128)(2,1)}, bf16[320,1792]{1,0:T(8,128)(2,1)}, u32[]{:S(2)}, u32[]{:S(2)}) collective-permute-start(bf16[320,1792]{1,0:T(8,128)(2,1)} %collective-permute-done), channel_id=1, source_target_pairs={{0,2},{2,4},{4,6},{6,0},{1,3},{3,5},{5,7},{7,1},{8,10},{10,12},{12... | collective-permute-start | bytes 3440648 | tf_op jit(solution)/shard_map/ppermute | solution.py:140
  246.6 29.1 %collective-permute-start.2 = (bf16[320,1792]{1,0:T(8,128)(2,1)}, bf16[320,1792]{1,0:T(8,128)(2,1)}, u32[]{:S(2)}, u32[]{:S(2)}) collective-permute-start(bf16[320,1792]{1,0:T(8,128)(2,1)} %collective-permute-done.1), channel_id=1, source_target_pairs={{0,2},{2,4},{4,6},{6,0},{1,3},{3,5},{5,7},{7,1},{8,10},{10,12},{12... | collective-permute-start | bytes 3440648 | tf_op jit(solution)/shard_map/ppermute | solution.py:140
  258.1 2.4 copy-start.2
  325.9 105.1 %copy-start.7 = (s32[2]{0:T(128)S(1)}, s32[2]{0:T(128)}, u32[]{:S(2)}) copy-start(s32[2]{0:T(128)} %param.22) | copy-start | bytes 28
Sparse Core Ops, SparseCore 0:
  10.1 160.6 all-gather.4
  186.0 131.3 all-gather.6
